TPU v7x, 64 devices: a 2x2x8 block of a 4x4x8 slice. The times are simulated.
64 devices in a mesh: dp: 4 (over x, y), sp: 16 (over z, core).
Axes of the slice: x: 2, y: 2, z: 8, core: 2. Of those that a mesh axis runs over, the one named last changes fastest.
The devices are a block of a 4x4x8 slice.
Arguments:
- q: bfloat16 [128, 56, 128], P('dp'), parts along dimension 0
- k: bfloat16 [128, 8192, 8, 128], P('dp', 'sp'), parts along dimension 0
- v: bfloat16 [128, 8192, 8, 128], P('dp', 'sp'), parts along dimension 0
Outputs:
- q: bfloat16 [128, 56, 128], P('dp'), parts along dimension 0
There are 4 independent parts. A program takes and returns all parts, laid end to end along the dimension named above; each array names one.
All inputs are finite; a program needn't handle non-finite values.
Results may differ from a plain program's by a relative error of at most 0.012.
Values are sent between devices in bfloat16 or wider.
A program may use at most 768 MiB of HBM per device.

v0:
```python
import jax
import jax.numpy as jnp
from jax import lax
from jax.sharding import PartitionSpec as P


def einsum(form, a, b):
    return jnp.einsum(form, a.astype(jnp.float32), b.astype(jnp.float32))


def part_of(q, k, v):
    grouped = q.reshape(q.shape[0], k.shape[2], -1, q.shape[2])
    scores = einsum("bgsd,bugd->bgsu", grouped, k) * q.shape[2] ** -0.5
    high = jnp.max(scores, -1, keepdims=True)
    weights = jnp.exp(scores - high)
    seen = einsum("bgsu,bugd->bgsd", weights.astype(jnp.bfloat16), v)
    return jnp.concatenate([seen, jnp.sum(weights, -1, keepdims=True), high], -1)


def together(parts):
    seen, total, high = parts[..., :-2], parts[..., -2:-1], parts[..., -1:]
    scale = jnp.exp(high - jnp.max(high, 0))
    return (jnp.sum(seen * scale, 0) / jnp.sum(total * scale, 0)).astype(jnp.bfloat16)


def solution(mesh):
    def step(q, k, v):
        return together(lax.all_gather(part_of(q, k, v), "sp")).reshape(q.shape)

    return jax.shard_map(
        step,
        mesh=mesh,
        in_specs=(P("dp", None, None), P("dp", "sp", None, None), P("dp", "sp", None, None)),
        out_specs=P("dp", None, None),
        check_vma=False,
    )
```

profile of v0, /device:TPU:21, one launch (start us, length us, event | category | flops | bytes accessed | tf_op | source)
XLA Modules:
  0.0 259.3 jit_solution(14065102980196960851)
XLA Ops:
  6.5 0.0 all-gather.3.cloned.1.call-start
  6.6 1.1 copy.46
  7.6 14.4 %multiply_reduce_fusion = (f32[32,8,7]{2,1,0:T(8,128)S(1)}, f32[32,8,7,512]{3,2,1,0:T(8,128)S(1)}) fusion(bf16[32,512,8,128]{3,2,1,0:T(8,128)(2,1)} %param.4, bf16[32,8,7,128]{3,0,2,1:T(8,128)(2,1)S(1)} %bitcast.14), kind=kOutput, calls=%fused_computation.7 | convolution fusion | flops 236714240 | bytes 37690368 | tf_op jit(solution)/shard_map/bgsd,bugd->bgsu/dot_general | solution.py:8
  22.0 0.0 copy-start
  22.0 1.9 copy-done
  24.0 1.2 fusion.5
  25.2 16.2 %fusion = f32[32,8,7,128]{3,2,1,0:T(8,128)S(1)} fusion(bf16[32,512,8,128]{3,2,1,0:T(8,128)(2,1)} %param.5, f32[32,8,7,512]{3,2,1,0:T(8,128)} %copy-done, f32[32,8,7]{2,1,0:T(8,128)S(1)} %get-tuple-element.10), kind=kOutput, calls=%fused_computation | convolution fusion | flops 237633536 | bytes 38149120 | tf_op jit(solution)/shard_map/bgsu,bugd->bgsd/dot_general | solution.py:8
  41.4 1.7 copy.52
  43.1 1.7 copy.53
  44.7 0.4 pad_maximum_fusion
  45.1 2.0 copy.54
  47.2 0.1 all-gather.3.cloned.1.call-update
  47.2 156.4 %all-gather.3.cloned.1.call-done = f32[512,8,7,130]{3,1,2,0:T(8,128)} async-done(((f32[32,8,7,130]{3,1,2,0:T(8,128)}), f32[512,8,7,130]{3,1,2,0:T(8,128)}) %all-gather.3.cloned.1.call-update) | async-done | bytes 14909456 | tf_op jit(solution)/shard_map/all_gather | solution.py:28
  203.7 19.9 %fusion.14 = (f32[16,32,8,7,1]{4,2,3,1,0:T(8,128)}, f32[32,8,7]{1,2,0:T(8,128)S(1)}, f32[16,32,8,7,1]{4,2,3,1,0:T(8,128)}) fusion(f32[16,32,8,7,130]{4,2,3,1,0:T(8,128)} %bitcast.12), kind=kLoop, calls=%fused_computation.21 | loop fusion | flops 26880 | bytes 465920 | tf_op jit(solution)/shard_map/slice | solution.py:21
  223.6 9.6 %copy.68 = f32[16,32,8,7,1]{1,2,4,3,0:T(8,128)S(1)} copy(f32[16,32,8,7,1]{4,2,3,1,0:T(8,128)} %get-tuple-element.5) | data formatting | bytes 229376
  233.2 0.1 copy.70
  233.3 9.6 %copy.67 = f32[16,32,8,7,1]{1,2,4,3,0:T(8,128)S(1)} copy(f32[16,32,8,7,1]{4,2,3,1,0:T(8,128)} %get-tuple-element.7) | data formatting | bytes 229376
  243.0 0.1 multiply_reduce_fusion.1
  243.1 0.7 copy.56
  243.8 7.2 %fusion.4 = f32[32,8,7,128]{3,1,2,0:T(8,128)S(1)} fusion(f32[16,32,8,7,130]{4,2,3,1,0:T(8,128)} %bitcast.13, f32[16,32,8,7]{2,3,1,0:T(8,128)S(1)} %copy.56), kind=kLoop, calls=%fused_computation.5 | loop fusion | flops 7110656 | bytes 15712256 | tf_op jit(solution)/shard_map/reduce_sum | solution.py:23
  251.0 0.2 copy.58
  251.2 0.3 fusion.10
  251.5 0.9 copy.61
  (2 shorter events, 0.0 us)
Async XLA Ops:
  6.5 197.1 %all-gather.3.cloned.1.call-start = ((), (), s32[]{:S(2)}) async-start(), calls=%async_computation | async-start | bytes 31195136 | tf_op jit(solution)/shard_map/all_gather | solution.py:28
  22.0 1.9 copy-start
Sparse Core Ops, SparseCore 0:
  47.4 156.2 all-gather.2
where the time goes:
time: 260 us; the launch traced here: 259 us
  waiting for transfers between devices  156 us (60%)
  matrix products  30.6 us (12%)
  local copies, waits for them, and re-layouts  29.6 us (11%)
  other arithmetic  29.1 us (11%)
  between operations  13.5 us (5%)
    all_gather x1, waiting for transfers between devices, step(): return together(lax.all_gather(part_of(q, k, v), 'sp')).reshape(q.shape)  156 us
    dot_general x2, matrix products, einsum(): return jnp.einsum(form, a.astype(jnp.float32), b.astype(jnp.float32))  30.6 us
    unnamed x6, local copies, waits for them, and re-layouts  22.4 us
    slice x1, other arithmetic, together(): seen, total, high = (parts[..., :-2], parts[..., -2:-1], parts[..., -1:])  19.9 us
    reduce_sum x1, other arithmetic, together(): jnp.sum(seen * scale, 0) / jnp.sum(total * scale, 0)  7.16 us
  transfers between devices with their start and end apart: 1, of which 1 were waited for; matrix products, arithmetic and copies ran while one was open for 0% of the time, Pallas kernels for 0%

commit v1 on v0

v1 whole, which is shorter than its diff:
```python
import functools
import math

import jax
import jax.numpy as jnp
from jax import lax
from jax.experimental import pallas as pl
from jax.experimental.pallas import tpu as pltpu
from jax.sharding import PartitionSpec as P

F32, BF16 = jnp.float32, jnp.bfloat16
MESH = pl.DeviceIdType.MESH
SLOTS = 5
CHUNK = 512
LANES = 128


def kernel(n, key_heads, q_hbm, k_hbm, v_hbm, o_ref, qv, kbuf, vbuf, s0, s1, qb0, qb1, stage, stage_ml, own_f, recv, recv_ml,
           qsem, ksem, vsem, osend, orecv, msend, mrecv, gsend, grecv):
    seqs, heads, head = qv.shape
    rounds = seqs // n
    rep = heads // key_heads
    side = LANES // 2
    half = kbuf.shape[1] // 2
    pieces = half // CHUNK
    scale = head**-0.5 * math.log2(math.e)
    me = lax.axis_index("sp")

    def owner(step):
        t = lax.rem(step, n)
        u, chips = t // 2, n // 2
        odd = lax.rem(u, 2)
        dz = chips // 2 + (u // 2) * (1 - odd) - ((u + 1) // 2) * odd
        z = lax.rem(me // 2 + dz, chips)
        core = lax.rem(lax.rem(me, 2) + 1 + t, 2)
        return 2 * z + core

    def sequence(step):
        return (step // n) * n + owner(step)

    def kcopy(step):
        slot = lax.rem(step, SLOTS)
        return pltpu.make_async_copy(k_hbm.at[sequence(step)], kbuf.at[slot], ksem.at[slot])

    def vcopy(step):
        slot = lax.rem(step, SLOTS)
        return pltpu.make_async_copy(v_hbm.at[sequence(step)], vbuf.at[slot], vsem.at[slot])

    def part_copies(step):
        to, r = owner(step), step // n
        return (
            pltpu.make_async_remote_copy(stage.at[step], recv.at[r, me], osend.at[step], orecv.at[r, me], device_id={"sp": to}, device_id_type=MESH),
            pltpu.make_async_remote_copy(stage_ml.at[step], recv_ml.at[r, me], msend.at[step], mrecv.at[r, me], device_id={"sp": to}, device_id_type=MESH),
        )

    def part_arrivals(r, source):
        return (
            pltpu.make_async_remote_copy(stage.at[0], recv.at[r, source], osend.at[0], orecv.at[r, source], device_id={"sp": source}, device_id_type=MESH),
            pltpu.make_async_remote_copy(stage_ml.at[0], recv_ml.at[r, source], msend.at[0], mrecv.at[r, source], device_id={"sp": source}, device_id_type=MESH),
        )

    def result_copy(r, to):
        at = r * n + me
        return pltpu.make_async_remote_copy(o_ref.at[at], o_ref.at[at], gsend.at[r, to], grecv.at[r, me], device_id={"sp": to}, device_id_type=MESH)

    def result_arrival(r, source):
        at = r * n + source
        return pltpu.make_async_remote_copy(o_ref.at[at], o_ref.at[at], gsend.at[r, source], grecv.at[r, source], device_id={"sp": source}, device_id_type=MESH)

    kcopy(0).start()
    qcopy = pltpu.make_async_copy(q_hbm, qv, qsem)
    qcopy.start()
    vcopy(0).start()
    for step in range(1, SLOTS):
        kcopy(step).start()
        vcopy(step).start()
    barrier = pltpu.get_barrier_semaphore()
    for far in range(1, n):
        pl.semaphore_signal(barrier, inc=1, device_id={"sp": lax.rem(me + far, n)}, device_id_type=MESH)
    for qb in (qb0, qb1):
        qb[...] = jnp.zeros(qb.shape, qb.dtype)
    for r in range(rounds):
        recv[r, me] = jnp.zeros((heads, head), BF16)

    def own_mask(rows):
        row = lax.rem(lax.broadcasted_iota(jnp.int32, (rows, LANES), 0), key_heads)
        lane = lax.rem(lax.broadcasted_iota(jnp.int32, (rows, LANES), 1), side)
        return (lane >= row * rep) & (lane < row * rep + rep)

    own8, own16 = own_mask(8), own_mask(16)

    def scores_start(step, qb):
        kcopy(step).wait()
        queries = qv[sequence(step)]
        qb[0:heads, 0:head] = queries
        qb[side : side + heads, head : 2 * head] = queries

    def scores_piece(step, piece, qb, s, high):
        slot = lax.rem(step, SLOTS)
        keys = jnp.concatenate([kbuf[slot, pl.ds(piece * CHUNK, CHUNK), :], kbuf[slot, pl.ds(half + piece * CHUNK, CHUNK), :]], axis=1)
        scores = lax.dot_general(keys, qb[...], (((1,), (1,)), ((), ())), preferred_element_type=F32)
        s[pl.ds(piece * CHUNK, CHUNK), :] = scores
        return jnp.maximum(high, jnp.max(scores.reshape(CHUNK // 8, 8, LANES), axis=0))

    def scores_end(high):
        high = jnp.max(jnp.where(own8, high, -jnp.inf), axis=0, keepdims=True)
        return jnp.maximum(high, pltpu.roll(high, side, 1))

    def values_piece(step, piece, s, high, total, seen):
        slot = lax.rem(step, SLOTS)
        weights = jnp.exp2(s[pl.ds(piece * CHUNK, CHUNK), :] * scale - high * scale)
        total = total + jnp.sum(weights.reshape(CHUNK // 8, 8, LANES), axis=0)
        rounded = weights.astype(BF16).reshape(CHUNK // 16, 16, LANES)
        rounded = jnp.where(own16[None], rounded, jnp.zeros_like(rounded)).reshape(CHUNK, LANES)
        values = jnp.concatenate([vbuf[slot, pl.ds(piece * CHUNK, CHUNK), :], vbuf[slot, pl.ds(half + piece * CHUNK, CHUNK), :]], axis=1)
        return total, seen + lax.dot_general(rounded, values, (((0,), (0,)), ((), ())), preferred_element_type=F32)

    def values_end(step, high, total, seen):
        total = jnp.sum(jnp.where(own8, total, 0.0), axis=0, keepdims=True)
        total = total + pltpu.roll(total, side, 1)
        seen = seen[0:heads, 0:head] + seen[side : side + heads, head : 2 * head]
        stage[step] = seen.astype(BF16)
        own_f[step // n] = seen
        stage_ml[step] = jnp.concatenate([high, total], axis=0)

    first = jnp.full((8, LANES), -jnp.inf, F32)
    zeros = (jnp.zeros((8, LANES), F32), jnp.zeros((2 * side, 2 * head), F32))

    def send(step):
        @pl.when(lax.rem(step, n) != n - 1)
        def _():
            for copy in part_copies(step):
                copy.start()

    def both(step, high, qb, s, s_before):
        scores_start(step, qb)
        vcopy(step - 1).wait()
        new, (total, seen) = first, zeros
        for piece in range(pieces):
            new = scores_piece(step, piece, qb, s, new)
            total, seen = values_piece(step - 1, piece, s_before, high, total, seen)
        values_end(step - 1, high, total, seen)
        return scores_end(new)

    def refill(step):
        @pl.when(step + SLOTS < seqs)
        def _():
            kcopy(step + SLOTS).start()

        @pl.when(step - 1 + SLOTS < seqs)
        def _():
            vcopy(step - 1 + SLOTS).start()

    def combine(r):
        recv_ml[r, me] = stage_ml[r * n + n - 1]
        for far in range(1, n):
            for copy in part_arrivals(r, lax.rem(me + far, n)):
                copy.wait_recv()
        high, total = recv_ml[r, :, 0, :], recv_ml[r, :, 1, :]
        highest = jnp.max(high, axis=0, keepdims=True)
        share = jnp.exp2(high * scale - highest * scale)
        whole = jnp.sum(share * total, axis=0, keepdims=True)
        mine = jnp.exp2(stage_ml[r * n + n - 1, 0:1, :] * scale - highest * scale)
        share = jnp.concatenate([share, jnp.broadcast_to(mine, (8, LANES))], axis=0) / whole
        share = jnp.concatenate([share, jnp.zeros((LANES - n - 8, LANES), F32)], axis=0).T
        result = share[0:heads, n : n + 1] * own_f[r]
        for source in range(n):
            result = result + share[0:heads, source : source + 1] * recv[r, source].astype(F32)
        o_ref[r * n + me] = result.astype(BF16)
        for far in range(1, n):
            result_copy(r, lax.rem(me + far, n)).start()

    qcopy.wait()
    scores_start(0, qb0)
    high = first
    for piece in range(pieces):
        high = scores_piece(0, piece, qb0, s0, high)
    high = scores_end(high)
    kcopy(SLOTS).start()
    pl.semaphore_wait(barrier, n - 1)

    def body(trip, high):
        step = 2 * trip + 1
        high = both(step, high, qb1, s1, s0)
        refill(step)

        @pl.when(trip >= 1)
        def _():
            send(step - 2)

        high = both(step + 1, high, qb0, s0, s1)
        refill(step + 1)
        send(step - 1)
        for r in range(rounds - 1):
            @pl.when(step + 1 == (r + 1) * n + 4)
            def _():
                combine(r)

        return high

    high = lax.fori_loop(0, (seqs - 2) // 2, body, high)
    send(seqs - 3)
    high = both(seqs - 1, high, qb1, s1, s0)
    send(seqs - 2)
    vcopy(seqs - 1).wait()
    total, seen = zeros
    for piece in range(pieces):
        total, seen = values_piece(seqs - 1, piece, s1, high, total, seen)
    values_end(seqs - 1, high, total, seen)
    combine(rounds - 1)

    def drain(step, _):
        @pl.when(lax.rem(step, n) != n - 1)
        def _():
            for copy in part_copies(step):
                copy.wait_send()

        return 0

    lax.fori_loop(0, seqs, drain, 0)
    for r in range(rounds):
        for far in range(1, n):
            other = lax.rem(me + far, n)
            result_copy(r, other).wait_send()
            result_arrival(r, other).wait_recv()


def solution(mesh):
    n = mesh.shape["sp"]

    def step(q, k, v):
        seqs, heads, head = q.shape
        tokens, key_heads = k.shape[1:3]
        rows = tokens * key_heads
        rounds = seqs // n
        anywhere = pl.BlockSpec(memory_space=pl.ANY)
        dma = pltpu.SemaphoreType.DMA
        return pl.pallas_call(
            functools.partial(kernel, n, key_heads),
            out_shape=jax.ShapeDtypeStruct(q.shape, BF16),
            in_specs=[anywhere] * 3,
            out_specs=pl.BlockSpec(memory_space=pltpu.VMEM),
            scratch_shapes=[
                pltpu.VMEM(q.shape, BF16),
                pltpu.VMEM((SLOTS, rows, head), BF16),
                pltpu.VMEM((SLOTS, rows, head), BF16),
                pltpu.VMEM((rows // 2, LANES), F32),
                pltpu.VMEM((rows // 2, LANES), F32),
                pltpu.VMEM((LANES, 2 * head), BF16),
                pltpu.VMEM((LANES, 2 * head), BF16),
                pltpu.VMEM((seqs, heads, head), BF16),
                pltpu.VMEM((seqs, 2, LANES), F32),
                pltpu.VMEM((rounds, heads, head), F32),
                pltpu.VMEM((rounds, n, heads, head), BF16),
                pltpu.VMEM((rounds, n, 2, LANES), F32),
                dma,
                dma((SLOTS,)),
                dma((SLOTS,)),
                dma((seqs,)),
                dma((rounds, n)),
                dma((seqs,)),
                dma((rounds, n)),
                dma((rounds, n)),
                dma((rounds, n)),
            ],
            compiler_params=pltpu.CompilerParams(collective_id=0, has_side_effects=True, vmem_limit_bytes=40 << 20),
        )(q, k.reshape(seqs, rows, head), v.reshape(seqs, rows, head))

    return jax.shard_map(
        step,
        mesh=mesh,
        in_specs=(P("dp", None, None), P("dp", "sp", None, None), P("dp", "sp", None, None)),
        out_specs=P("dp", None, None),
        check_vma=False,
    )
```

time: 260 us -> 50.8 us (0.20)
  waiting for transfers between devices: 156 us -> 0 us
  Pallas kernels: 0 us -> 48.9 us
  matrix products: 30.6 us -> 0 us
  other arithmetic: 29.1 us -> 0 us
  local copies, waits for them, and re-layouts: 29.6 us -> 1.79 us
  between operations: 13.5 us -> 0.01 us
    all_gather x1 -> x0, waiting for transfers between devices: 156 us -> none  [step(): return together(lax.all_gather(part_of(q, k, v), 'sp')).reshape(q.shape)]
    pallas_call x0 -> x1, Pallas kernels: none -> 48.9 us  [step(): pl.pallas_call(functools.partial(kernel, n, key_heads), out_shape=jax.Sha...]
    dot_general x2 -> x0, matrix products: 30.6 us -> none  [einsum(): return jnp.einsum(form, a.astype(jnp.float32), b.astype(jnp.float32))]
    unnamed x6 -> x3, local copies, waits for them, and re-layouts: 22.4 us -> 1.79 us
    slice x1 -> x0, other arithmetic: 19.9 us -> none  [together(): seen, total, high = (parts[..., :-2], parts[..., -2:-1], parts[..., -1:])]
    reduce_sum x3 -> x0, other arithmetic: 8.43 us -> none  [the longest x1 7.16 us: together(): jnp.sum(seen * scale, 0) / jnp.sum(total * scale, 0)]
    broadcast_in_dim x2 -> x0, local copies, waits for them, and re-layouts: 3.33 us -> none  [the longest x1 1.66 us: part_of(): jnp.sum(weights, -1, keepdims=True)]
  transfers between devices with their start and end apart: 1 -> 0, of which waited for: 1 -> 0; matrix products, arithmetic and copies ran while one was open for 0% -> 0% of each run, Pallas kernels for 0% -> 0%
where the time goes in v1:
time: 50.8 us; the launch traced here: 50.7 us
  Pallas kernels  48.9 us (96%)
  local copies, waits for them, and re-layouts  1.79 us (4%)
    pallas_call x1, Pallas kernels, step(): pl.pallas_call(functools.partial(kernel, n, key_heads), out_shape=jax.Sha...  48.9 us
    unnamed x3, local copies, waits for them, and re-layouts  1.79 us

profile of v1, /device:TPU:21, one launch (start us, length us, event | category | flops | bytes accessed | tf_op | source)
XLA Modules:
  0.0 50.7 jit_solution(4499053243449286486)
XLA Ops:
  0.0 0.0 copy-start
  0.0 1.0 %copy-done = bf16[32,56,128]{2,1,0:T(8,128)(2,1)S(1)} copy-done((bf16[32,56,128]{2,1,0:T(8,128)(2,1)S(1)}, bf16[32,56,128]{2,1,0:T(8,128)(2,1)}, u32[]{:S(2)}) %copy-start) | copy-done | bytes 458776
  1.0 48.9 %shard_map.37 = bf16[32,56,128]{2,1,0:T(8,128)(2,1)S(1)} custom-call(bf16[32,56,128]{2,1,0:T(8,128)(2,1)S(1)} %copy-done, bf16[32,4096,128]{2,1,0:T(8,128)(2,1)} %bitcast.2, bf16[32,4096,128]{2,1,0:T(8,128)(2,1)} %bitcast.3), custom_call_target="tpu_custom_call" | custom-call | tf_op jit(solution)/shard_map/pallas_call | solution.py:238
  49.9 0.8 %copy.5 = bf16[32,56,128]{2,1,0:T(8,128)(2,1)} copy(bf16[32,56,128]{2,1,0:T(8,128)(2,1)S(1)} %shard_map.37) | data formatting | bytes 917504
Async XLA Ops:
  0.0 1.0 %copy-start = (bf16[32,56,128]{2,1,0:T(8,128)(2,1)S(1)}, bf16[32,56,128]{2,1,0:T(8,128)(2,1)}, u32[]{:S(2)}) copy-start(bf16[32,56,128]{2,1,0:T(8,128)(2,1)} %q_hbm.1) | copy-start | bytes 1376260

commit v2 on v1

--- a/solution.py
+++ b/solution.py
@@ -10,13 +10,13 @@
 
 F32, BF16 = jnp.float32, jnp.bfloat16
 MESH = pl.DeviceIdType.MESH
-SLOTS = 5
-CHUNK = 512
+SLOTS = 8
+CHUNK = 1024
 LANES = 128
 
 
 def kernel(n, key_heads, q_hbm, k_hbm, v_hbm, o_ref, qv, kbuf, vbuf, s0, s1, qb0, qb1, stage, stage_ml, own_f, recv, recv_ml,
-           qsem, ksem, vsem, osend, orecv, msend, mrecv, gsend, grecv):
+           qsem, ksem, vsem, osend, orecv, msend, mrecv, gsend, grecv, fsend, frecv):
     seqs, heads, head = qv.shape
     rounds = seqs // n
     rep = heads // key_heads
@@ -26,14 +26,19 @@
     scale = head**-0.5 * math.log2(math.e)
     me = lax.axis_index("sp")
 
+    chips = n // 2
+    partner = 2 * (me // 2) + 1 - lax.rem(me, 2)
+
+    def ahead(u):
+        odd = u % 2
+        return chips // 2 + (u // 2) * (1 - odd) - ((u + 1) // 2) * odd
+
+    def device(dz, other):
+        return 2 * lax.rem(me // 2 + dz, chips) + lax.rem(lax.rem(me, 2) + other, 2)
+
     def owner(step):
         t = lax.rem(step, n)
-        u, chips = t // 2, n // 2
-        odd = lax.rem(u, 2)
-        dz = chips // 2 + (u // 2) * (1 - odd) - ((u + 1) // 2) * odd
-        z = lax.rem(me // 2 + dz, chips)
-        core = lax.rem(lax.rem(me, 2) + 1 + t, 2)
-        return 2 * z + core
+        return device(ahead(t // 2), 1 - lax.rem(t, 2))
 
     def sequence(step):
         return (step // n) * n + owner(step)
@@ -47,25 +52,29 @@
         return pltpu.make_async_copy(v_hbm.at[sequence(step)], vbuf.at[slot], vsem.at[slot])
 
     def part_copies(step):
-        to, r = owner(step), step // n
+        to, r, t = owner(step), step // n, lax.rem(step, n)
         return (
-            pltpu.make_async_remote_copy(stage.at[step], recv.at[r, me], osend.at[step], orecv.at[r, me], device_id={"sp": to}, device_id_type=MESH),
-            pltpu.make_async_remote_copy(stage_ml.at[step], recv_ml.at[r, me], msend.at[step], mrecv.at[r, me], device_id={"sp": to}, device_id_type=MESH),
+            pltpu.make_async_remote_copy(stage.at[step], recv.at[r, t], osend.at[step], orecv.at[r, t], device_id={"sp": to}, device_id_type=MESH),
+            pltpu.make_async_remote_copy(stage_ml.at[step], recv_ml.at[r, t], msend.at[step], mrecv.at[r, t], device_id={"sp": to}, device_id_type=MESH),
         )
 
-    def part_arrivals(r, source):
-        return (
-            pltpu.make_async_remote_copy(stage.at[0], recv.at[r, source], osend.at[0], orecv.at[r, source], device_id={"sp": source}, device_id_type=MESH),
-            pltpu.make_async_remote_copy(stage_ml.at[0], recv_ml.at[r, source], msend.at[0], mrecv.at[r, source], device_id={"sp": source}, device_id_type=MESH),
-        )
-
-    def result_copy(r, to):
+    def result_copy(r, u):
         at = r * n + me
-        return pltpu.make_async_remote_copy(o_ref.at[at], o_ref.at[at], gsend.at[r, to], grecv.at[r, me], device_id={"sp": to}, device_id_type=MESH)
-
-    def result_arrival(r, source):
+        to = device(ahead(u), 0) if u < chips - 1 else partner
+        return pltpu.make_async_remote_copy(o_ref.at[at], o_ref.at[at], gsend.at[r, u], grecv.at[r, u], device_id={"sp": to}, device_id_type=MESH)
+
+    def result_arrival(r, u):
+        source = device(chips - ahead(u), 0) if u < chips - 1 else partner
         at = r * n + source
-        return pltpu.make_async_remote_copy(o_ref.at[at], o_ref.at[at], gsend.at[r, source], grecv.at[r, source], device_id={"sp": source}, device_id_type=MESH)
+        return pltpu.make_async_remote_copy(o_ref.at[at], o_ref.at[at], gsend.at[r, u], grecv.at[r, u], device_id={"sp": source}, device_id_type=MESH)
+
+    def forward_copy(r, u):
+        at = r * n + device(chips - ahead(u), 0)
+        return pltpu.make_async_remote_copy(o_ref.at[at], o_ref.at[at], fsend.at[r, u], frecv.at[r, u], device_id={"sp": partner}, device_id_type=MESH)
+
+    def forward_arrival(r, u):
+        at = r * n + device(chips - ahead(u), 1)
+        return pltpu.make_async_remote_copy(o_ref.at[at], o_ref.at[at], fsend.at[r, u], frecv.at[r, u], device_id={"sp": partner}, device_id_type=MESH)
 
     kcopy(0).start()
     qcopy = pltpu.make_async_copy(q_hbm, qv, qsem)
@@ -79,8 +88,6 @@
         pl.semaphore_signal(barrier, inc=1, device_id={"sp": lax.rem(me + far, n)}, device_id_type=MESH)
     for qb in (qb0, qb1):
         qb[...] = jnp.zeros(qb.shape, qb.dtype)
-    for r in range(rounds):
-        recv[r, me] = jnp.zeros((heads, head), BF16)
 
     def own_mask(rows):
         row = lax.rem(lax.broadcasted_iota(jnp.int32, (rows, LANES), 0), key_heads)
@@ -90,7 +97,6 @@
     own8, own16 = own_mask(8), own_mask(16)
 
     def scores_start(step, qb):
-        kcopy(step).wait()
         queries = qv[sequence(step)]
         qb[0:heads, 0:head] = queries
         qb[side : side + heads, head : 2 * head] = queries
@@ -134,7 +140,6 @@
 
     def both(step, high, qb, s, s_before):
         scores_start(step, qb)
-        vcopy(step - 1).wait()
         new, (total, seen) = first, zeros
         for piece in range(pieces):
             new = scores_piece(step, piece, qb, s, new)
@@ -152,24 +157,31 @@
             vcopy(step - 1 + SLOTS).start()
 
     def combine(r):
-        recv_ml[r, me] = stage_ml[r * n + n - 1]
-        for far in range(1, n):
-            for copy in part_arrivals(r, lax.rem(me + far, n)):
+        step = r * n + n - 1
+        for t in range(n - 2):
+            for copy in part_copies(r * n + t):
                 copy.wait_recv()
-        high, total = recv_ml[r, :, 0, :], recv_ml[r, :, 1, :]
-        highest = jnp.max(high, axis=0, keepdims=True)
-        share = jnp.exp2(high * scale - highest * scale)
-        whole = jnp.sum(share * total, axis=0, keepdims=True)
-        mine = jnp.exp2(stage_ml[r * n + n - 1, 0:1, :] * scale - highest * scale)
-        share = jnp.concatenate([share, jnp.broadcast_to(mine, (8, LANES))], axis=0) / whole
-        share = jnp.concatenate([share, jnp.zeros((LANES - n - 8, LANES), F32)], axis=0).T
-        result = share[0:heads, n : n + 1] * own_f[r]
-        for source in range(n):
-            result = result + share[0:heads, source : source + 1] * recv[r, source].astype(F32)
-        o_ref[r * n + me] = result.astype(BF16)
-        for far in range(1, n):
-            result_copy(r, lax.rem(me + far, n)).start()
-
+        high = recv_ml[r, 0 : n - 2, 0, :]
+        others = jnp.max(high, axis=0, keepdims=True)
+        share = jnp.exp2(high * scale - others * scale)
+        total = jnp.sum(share * recv_ml[r, 0 : n - 2, 1, :], axis=0, keepdims=True)
+        share = jnp.concatenate([share, jnp.zeros((LANES - (n - 2), LANES), F32)], axis=0).T
+        seen = share[0:heads, 0:1] * recv[r, 0].astype(F32)
+        for t in range(1, n - 2):
+            seen = seen + share[0:heads, t : t + 1] * recv[r, t].astype(F32)
+        for copy in part_copies(r * n + n - 2):
+            copy.wait_recv()
+        high = jnp.concatenate([others, recv_ml[r, n - 2, 0:1, :], stage_ml[step, 0:1, :]], axis=0)
+        total = jnp.concatenate([total, recv_ml[r, n - 2, 1:2, :], stage_ml[step, 1:2, :]], axis=0)
+        share = jnp.exp2(high * scale - jnp.max(high, axis=0, keepdims=True) * scale)
+        share = share / jnp.sum(share * total, axis=0, keepdims=True)
+        share = jnp.concatenate([share, jnp.zeros((LANES - 3, LANES), F32)], axis=0).T
+        seen = share[0:heads, 0:1] * seen + share[0:heads, 1:2] * recv[r, n - 2].astype(F32) + share[0:heads, 2:3] * own_f[r]
+        o_ref[r * n + me] = seen.astype(BF16)
+        for u in range(chips):
+            result_copy(r, u).start()
+
+    kcopy(0).wait()
     qcopy.wait()
     scores_start(0, qb0)
     high = first
@@ -181,15 +193,19 @@
 
     def body(trip, high):
         step = 2 * trip + 1
+        kcopy(step).wait()
+        vcopy(step - 1).wait()
+        kcopy(step + 1).wait()
+        vcopy(step).wait()
         high = both(step, high, qb1, s1, s0)
+        high = both(step + 1, high, qb0, s0, s1)
         refill(step)
+        refill(step + 1)
 
         @pl.when(trip >= 1)
         def _():
             send(step - 2)
 
-        high = both(step + 1, high, qb0, s0, s1)
-        refill(step + 1)
         send(step - 1)
         for r in range(rounds - 1):
             @pl.when(step + 1 == (r + 1) * n + 4)
@@ -200,6 +216,8 @@
 
     high = lax.fori_loop(0, (seqs - 2) // 2, body, high)
     send(seqs - 3)
+    kcopy(seqs - 1).wait()
+    vcopy(seqs - 2).wait()
     high = both(seqs - 1, high, qb1, s1, s0)
     send(seqs - 2)
     vcopy(seqs - 1).wait()
@@ -219,10 +237,16 @@
 
     lax.fori_loop(0, seqs, drain, 0)
     for r in range(rounds):
-        for far in range(1, n):
-            other = lax.rem(me + far, n)
-            result_copy(r, other).wait_send()
-            result_arrival(r, other).wait_recv()
+        for u in reversed(range(chips - 1)):
+            result_arrival(r, u).wait_recv()
+            forward_copy(r, u).start()
+    for r in range(rounds):
+        result_arrival(r, chips - 1).wait_recv()
+        for u in range(chips):
+            result_copy(r, u).wait_send()
+        for u in range(chips - 1):
+            forward_copy(r, u).wait_send()
+            forward_arrival(r, u).wait_recv()
 
 
 def solution(mesh):
@@ -233,12 +257,12 @@
         tokens, key_heads = k.shape[1:3]
         rows = tokens * key_heads
         rounds = seqs // n
-        anywhere = pl.BlockSpec(memory_space=pl.ANY)
+        in_hbm = pl.BlockSpec(memory_space=pltpu.HBM)
         dma = pltpu.SemaphoreType.DMA
         return pl.pallas_call(
             functools.partial(kernel, n, key_heads),
             out_shape=jax.ShapeDtypeStruct(q.shape, BF16),
-            in_specs=[anywhere] * 3,
+            in_specs=[in_hbm] * 3,
             out_specs=pl.BlockSpec(memory_space=pltpu.VMEM),
             scratch_shapes=[
                 pltpu.VMEM(q.shape, BF16),
@@ -260,11 +284,13 @@
                 dma((rounds, n)),
                 dma((seqs,)),
                 dma((rounds, n)),
-                dma((rounds, n)),
-                dma((rounds, n)),
+                dma((rounds, n // 2)),
+                dma((rounds, n // 2)),
+                dma((rounds, n // 2)),
+                dma((rounds, n // 2)),
             ],
-            compiler_params=pltpu.CompilerParams(collective_id=0, has_side_effects=True, vmem_limit_bytes=40 << 20),
-        )(q, k.reshape(seqs, rows, head), v.reshape(seqs, rows, head))
+            compiler_params=pltpu.CompilerParams(collective_id=0, has_side_effects=True, vmem_limit_bytes=48 << 20),
+        )(pltpu.with_memory_space_constraint(q, pltpu.HBM), k.reshape(seqs, rows, head), v.reshape(seqs, rows, head))
 
     return jax.shard_map(
         step,

time: 50.8 us -> 45.5 us (0.90)
  Pallas kernels: 48.9 us -> 44.7 us
  local copies, waits for them, and re-layouts: 1.79 us -> 0.77 us
    pallas_call x1, Pallas kernels: 48.9 us -> 44.7 us  [step(): pl.pallas_call(functools.partial(kernel, n, key_heads), out_shape=jax.Sha...]
    unnamed x3 -> x1, local copies, waits for them, and re-layouts: 1.79 us -> 0.77 us
where the time goes in v2:
time: 45.5 us
  Pallas kernels  44.7 us (98%)
  local copies, waits for them, and re-layouts  0.77 us (2%)
    pallas_call x1, Pallas kernels, step(): pl.pallas_call(functools.partial(kernel, n, key_heads), out_shape=jax.Sha...  44.7 us

profile of v2, /device:TPU:21, one launch (start us, length us, event | category | flops | bytes accessed | tf_op | source)
XLA Modules:
  0.0 45.5 jit_solution(13061374614260042530)
XLA Ops:
  0.0 44.7 %shard_map.37 = bf16[32,56,128]{2,1,0:T(8,128)(2,1)S(1)} custom-call(bf16[32,56,128]{2,1,0:T(8,128)(2,1)} %q_hbm.1, bf16[32,4096,128]{2,1,0:T(8,128)(2,1)} %bitcast.2, bf16[32,4096,128]{2,1,0:T(8,128)(2,1)} %bitcast.3), custom_call_target="tpu_custom_call" | custom-call | tf_op jit(solution)/shard_map/pallas_call | solution.py:262
  44.7 0.8 %copy.5 = bf16[32,56,128]{2,1,0:T(8,128)(2,1)} copy(bf16[32,56,128]{2,1,0:T(8,128)(2,1)S(1)} %shard_map.37) | data formatting | bytes 917504

commit v3 on v2

--- a/solution.py
+++ b/solution.py
@@ -10,7 +10,7 @@
 
 F32, BF16 = jnp.float32, jnp.bfloat16
 MESH = pl.DeviceIdType.MESH
-SLOTS = 8
+SLOTS = 6
 CHUNK = 1024
 LANES = 128
 
@@ -76,13 +76,11 @@
         at = r * n + device(chips - ahead(u), 1)
         return pltpu.make_async_remote_copy(o_ref.at[at], o_ref.at[at], fsend.at[r, u], frecv.at[r, u], device_id={"sp": partner}, device_id_type=MESH)
 
-    kcopy(0).start()
     qcopy = pltpu.make_async_copy(q_hbm, qv, qsem)
     qcopy.start()
+    kcopy(0).start()
+    kcopy(1).start()
     vcopy(0).start()
-    for step in range(1, SLOTS):
-        kcopy(step).start()
-        vcopy(step).start()
     barrier = pltpu.get_barrier_semaphore()
     for far in range(1, n):
         pl.semaphore_signal(barrier, inc=1, device_id={"sp": lax.rem(me + far, n)}, device_id_type=MESH)
@@ -148,13 +146,14 @@
         return scores_end(new)
 
     def refill(step):
-        @pl.when(step + SLOTS < seqs)
-        def _():
-            kcopy(step + SLOTS).start()
-
-        @pl.when(step - 1 + SLOTS < seqs)
-        def _():
-            vcopy(step - 1 + SLOTS).start()
+        for at in (step, step + 1):
+            @pl.when(at < seqs)
+            def _():
+                kcopy(at).start()
+
+            @pl.when(at - 1 < seqs)
+            def _():
+                vcopy(at - 1).start()
 
     def combine(r):
         step = r * n + n - 1
@@ -183,12 +182,14 @@
 
     kcopy(0).wait()
     qcopy.wait()
+    for step in (2, 3, 4):
+        kcopy(step).start()
+        vcopy(step - 1).start()
     scores_start(0, qb0)
     high = first
     for piece in range(pieces):
         high = scores_piece(0, piece, qb0, s0, high)
     high = scores_end(high)
-    kcopy(SLOTS).start()
     pl.semaphore_wait(barrier, n - 1)
 
     def body(trip, high):
@@ -197,10 +198,9 @@
         vcopy(step - 1).wait()
         kcopy(step + 1).wait()
         vcopy(step).wait()
+        refill(step + 4)
         high = both(step, high, qb1, s1, s0)
         high = both(step + 1, high, qb0, s0, s1)
-        refill(step)
-        refill(step + 1)
 
         @pl.when(trip >= 1)
         def _():

time: 45.5 us -> 43.5 us (0.956)
  Pallas kernels: 44.7 us -> 42.7 us
    pallas_call x1, Pallas kernels: 44.7 us -> 42.7 us  [step(): pl.pallas_call(functools.partial(kernel, n, key_heads), out_shape=jax.Sha...]
where the time goes in v3:
time: 43.5 us; the launch traced here: 43.4 us
  Pallas kernels  42.7 us (98%)
  local copies, waits for them, and re-layouts  0.77 us (2%)
    pallas_call x1, Pallas kernels, step(): pl.pallas_call(functools.partial(kernel, n, key_heads), out_shape=jax.Sha...  42.7 us

profile of v3, /device:TPU:21, one launch (start us, length us, event | category | flops | bytes accessed | tf_op | source)
XLA Modules:
  0.0 43.4 jit_solution(16919427865941272840)
XLA Ops:
  0.0 42.7 %shard_map.37 = bf16[32,56,128]{2,1,0:T(8,128)(2,1)S(1)} custom-call(bf16[32,56,128]{2,1,0:T(8,128)(2,1)} %q_hbm.1, bf16[32,4096,128]{2,1,0:T(8,128)(2,1)} %bitcast.2, bf16[32,4096,128]{2,1,0:T(8,128)(2,1)} %bitcast.3), custom_call_target="tpu_custom_call" | custom-call | tf_op jit(solution)/shard_map/pallas_call | solution.py:262
  42.7 0.8 %copy.5 = bf16[32,56,128]{2,1,0:T(8,128)(2,1)} copy(bf16[32,56,128]{2,1,0:T(8,128)(2,1)S(1)} %shard_map.37) | data formatting | bytes 917504

commit v4 on v3

--- a/solution.py
+++ b/solution.py
@@ -10,9 +10,17 @@
 
 F32, BF16 = jnp.float32, jnp.bfloat16
 MESH = pl.DeviceIdType.MESH
-SLOTS = 6
+SLOTS = 8
 CHUNK = 1024
 LANES = 128
+
+
+def rest(x, by):
+    return x & (by - 1) if by & (by - 1) == 0 else lax.rem(x, by)
+
+
+def whole(x, by):
+    return x >> (by.bit_length() - 1) if by & (by - 1) == 0 else lax.div(x, by)
 
 
 def kernel(n, key_heads, q_hbm, k_hbm, v_hbm, o_ref, qv, kbuf, vbuf, s0, s1, qb0, qb1, stage, stage_ml, own_f, recv, recv_ml,
@@ -27,32 +35,40 @@
     me = lax.axis_index("sp")
 
     chips = n // 2
-    partner = 2 * (me // 2) + 1 - lax.rem(me, 2)
+    partner = me + 1 - 2 * rest(me, 2)
 
     def ahead(u):
-        odd = u % 2
-        return chips // 2 + (u // 2) * (1 - odd) - ((u + 1) // 2) * odd
+        near, odd = (u // 2, u % 2) if isinstance(u, int) else (whole(u, 2), rest(u, 2))
+        return chips // 2 + near - (2 * near + 1) * odd
 
     def device(dz, other):
-        return 2 * lax.rem(me // 2 + dz, chips) + lax.rem(lax.rem(me, 2) + other, 2)
+        return 2 * rest(whole(me, 2) + dz, chips) + rest(rest(me, 2) + other, 2)
+
+    def place(step):
+        last = rounds * (n - 1)
+        if isinstance(step, int):
+            return (step // (n - 1), step % (n - 1)) if step < last else (step - last, n - 1)
+        r = (step >= n - 1).astype(jnp.int32)
+        own = (step >= last).astype(jnp.int32)
+        return (1 - own) * r + own * (step - last), (1 - own) * (step - (n - 1) * r) + own * (n - 1)
 
     def owner(step):
-        t = lax.rem(step, n)
-        return device(ahead(t // 2), 1 - lax.rem(t, 2))
+        _, t = place(step)
+        return device(ahead(whole(t, 2)), 1 - rest(t, 2))
 
     def sequence(step):
-        return (step // n) * n + owner(step)
+        return place(step)[0] * n + owner(step)
 
     def kcopy(step):
-        slot = lax.rem(step, SLOTS)
+        slot = rest(step, SLOTS)
         return pltpu.make_async_copy(k_hbm.at[sequence(step)], kbuf.at[slot], ksem.at[slot])
 
     def vcopy(step):
-        slot = lax.rem(step, SLOTS)
+        slot = rest(step, SLOTS)
         return pltpu.make_async_copy(v_hbm.at[sequence(step)], vbuf.at[slot], vsem.at[slot])
 
     def part_copies(step):
-        to, r, t = owner(step), step // n, lax.rem(step, n)
+        (r, t), to = place(step), owner(step)
         return (
             pltpu.make_async_remote_copy(stage.at[step], recv.at[r, t], osend.at[step], orecv.at[r, t], device_id={"sp": to}, device_id_type=MESH),
             pltpu.make_async_remote_copy(stage_ml.at[step], recv_ml.at[r, t], msend.at[step], mrecv.at[r, t], device_id={"sp": to}, device_id_type=MESH),
@@ -79,8 +95,9 @@
     qcopy = pltpu.make_async_copy(q_hbm, qv, qsem)
     qcopy.start()
     kcopy(0).start()
-    kcopy(1).start()
-    vcopy(0).start()
+    for step in (1, 2):
+        kcopy(step).start()
+        vcopy(step - 1).start()
     barrier = pltpu.get_barrier_semaphore()
     for far in range(1, n):
         pl.semaphore_signal(barrier, inc=1, device_id={"sp": lax.rem(me + far, n)}, device_id_type=MESH)
@@ -100,7 +117,7 @@
         qb[side : side + heads, head : 2 * head] = queries
 
     def scores_piece(step, piece, qb, s, high):
-        slot = lax.rem(step, SLOTS)
+        slot = rest(step, SLOTS)
         keys = jnp.concatenate([kbuf[slot, pl.ds(piece * CHUNK, CHUNK), :], kbuf[slot, pl.ds(half + piece * CHUNK, CHUNK), :]], axis=1)
         scores = lax.dot_general(keys, qb[...], (((1,), (1,)), ((), ())), preferred_element_type=F32)
         s[pl.ds(piece * CHUNK, CHUNK), :] = scores
@@ -111,7 +128,7 @@
         return jnp.maximum(high, pltpu.roll(high, side, 1))
 
     def values_piece(step, piece, s, high, total, seen):
-        slot = lax.rem(step, SLOTS)
+        slot = rest(step, SLOTS)
         weights = jnp.exp2(s[pl.ds(piece * CHUNK, CHUNK), :] * scale - high * scale)
         total = total + jnp.sum(weights.reshape(CHUNK // 8, 8, LANES), axis=0)
         rounded = weights.astype(BF16).reshape(CHUNK // 16, 16, LANES)
@@ -124,14 +141,14 @@
         total = total + pltpu.roll(total, side, 1)
         seen = seen[0:heads, 0:head] + seen[side : side + heads, head : 2 * head]
         stage[step] = seen.astype(BF16)
-        own_f[step // n] = seen
+        own_f[step & 1] = seen
         stage_ml[step] = jnp.concatenate([high, total], axis=0)
 
     first = jnp.full((8, LANES), -jnp.inf, F32)
     zeros = (jnp.zeros((8, LANES), F32), jnp.zeros((2 * side, 2 * head), F32))
 
     def send(step):
-        @pl.when(lax.rem(step, n) != n - 1)
+        @pl.when(step < rounds * (n - 1))
         def _():
             for copy in part_copies(step):
                 copy.start()
@@ -156,9 +173,9 @@
                 vcopy(at - 1).start()
 
     def combine(r):
-        step = r * n + n - 1
+        step = rounds * (n - 1) + r
         for t in range(n - 2):
-            for copy in part_copies(r * n + t):
+            for copy in part_copies(r * (n - 1) + t):
                 copy.wait_recv()
         high = recv_ml[r, 0 : n - 2, 0, :]
         others = jnp.max(high, axis=0, keepdims=True)
@@ -168,7 +185,7 @@
         seen = share[0:heads, 0:1] * recv[r, 0].astype(F32)
         for t in range(1, n - 2):
             seen = seen + share[0:heads, t : t + 1] * recv[r, t].astype(F32)
-        for copy in part_copies(r * n + n - 2):
+        for copy in part_copies(r * (n - 1) + n - 2):
             copy.wait_recv()
         high = jnp.concatenate([others, recv_ml[r, n - 2, 0:1, :], stage_ml[step, 0:1, :]], axis=0)
         total = jnp.concatenate([total, recv_ml[r, n - 2, 1:2, :], stage_ml[step, 1:2, :]], axis=0)
@@ -182,7 +199,7 @@
 
     kcopy(0).wait()
     qcopy.wait()
-    for step in (2, 3, 4):
+    for step in (3, 4, 5):
         kcopy(step).start()
         vcopy(step - 1).start()
     scores_start(0, qb0)
@@ -198,7 +215,7 @@
         vcopy(step - 1).wait()
         kcopy(step + 1).wait()
         vcopy(step).wait()
-        refill(step + 4)
+        refill(step + 5)
         high = both(step, high, qb1, s1, s0)
         high = both(step + 1, high, qb0, s0, s1)
 
@@ -207,11 +224,6 @@
             send(step - 2)
 
         send(step - 1)
-        for r in range(rounds - 1):
-            @pl.when(step + 1 == (r + 1) * n + 4)
-            def _():
-                combine(r)
-
         return high
 
     high = lax.fori_loop(0, (seqs - 2) // 2, body, high)
@@ -219,7 +231,7 @@
     kcopy(seqs - 1).wait()
     vcopy(seqs - 2).wait()
     high = both(seqs - 1, high, qb1, s1, s0)
-    send(seqs - 2)
+    combine(0)
     vcopy(seqs - 1).wait()
     total, seen = zeros
     for piece in range(pieces):
@@ -228,7 +240,7 @@
     combine(rounds - 1)
 
     def drain(step, _):
-        @pl.when(lax.rem(step, n) != n - 1)
+        @pl.when(step < rounds * (n - 1))
         def _():
             for copy in part_copies(step):
                 copy.wait_send()

time: 43.5 us -> 40.6 us (0.933)
  Pallas kernels: 42.7 us -> 39.7 us
    pallas_call x1, Pallas kernels: 42.7 us -> 39.7 us  [step(): pl.pallas_call(functools.partial(kernel, n, key_heads), out_shape=jax.Sha...]
where the time goes in v4:
time: 40.6 us; the launch traced here: 40.5 us
  Pallas kernels  39.7 us (98%)
  local copies, waits for them, and re-layouts  0.77 us (2%)
    pallas_call x1, Pallas kernels, step(): pl.pallas_call(functools.partial(kernel, n, key_heads), out_shape=jax.Sha...  39.7 us

profile of v4, /device:TPU:21, one launch (start us, length us, event | category | flops | bytes accessed | tf_op | source)
XLA Modules:
  0.0 40.5 jit_solution(4767474058727516982)
XLA Ops:
  0.0 39.7 %shard_map.37 = bf16[32,56,128]{2,1,0:T(8,128)(2,1)S(1)} custom-call(bf16[32,56,128]{2,1,0:T(8,128)(2,1)} %q_hbm.1, bf16[32,4096,128]{2,1,0:T(8,128)(2,1)} %bitcast.2, bf16[32,4096,128]{2,1,0:T(8,128)(2,1)} %bitcast.3), custom_call_target="tpu_custom_call" | custom-call | tf_op jit(solution)/shard_map/pallas_call | solution.py:274
  39.8 0.8 %copy.5 = bf16[32,56,128]{2,1,0:T(8,128)(2,1)} copy(bf16[32,56,128]{2,1,0:T(8,128)(2,1)S(1)} %shard_map.37) | data formatting | bytes 917504

commit v5 on v4

--- a/solution.py
+++ b/solution.py
@@ -13,6 +13,7 @@
 SLOTS = 8
 CHUNK = 1024
 LANES = 128
+QUIET = 4
 
 
 def rest(x, by):
@@ -45,16 +46,11 @@
         return 2 * rest(whole(me, 2) + dz, chips) + rest(rest(me, 2) + other, 2)
 
     def place(step):
-        last = rounds * (n - 1)
-        if isinstance(step, int):
-            return (step // (n - 1), step % (n - 1)) if step < last else (step - last, n - 1)
-        r = (step >= n - 1).astype(jnp.int32)
-        own = (step >= last).astype(jnp.int32)
-        return (1 - own) * r + own * (step - last), (1 - own) * (step - (n - 1) * r) + own * (n - 1)
+        return (step % rounds, step // rounds) if isinstance(step, int) else (rest(step, rounds), whole(step, rounds))
 
     def owner(step):
         _, t = place(step)
-        return device(ahead(whole(t, 2)), 1 - rest(t, 2))
+        return device(ahead(t // 2 if isinstance(t, int) else whole(t, 2)), 1 - rest(t, 2))
 
     def sequence(step):
         return place(step)[0] * n + owner(step)
@@ -67,11 +63,11 @@
         slot = rest(step, SLOTS)
         return pltpu.make_async_copy(v_hbm.at[sequence(step)], vbuf.at[slot], vsem.at[slot])
 
-    def part_copies(step):
-        (r, t), to = place(step), owner(step)
+    def part_copies(t):
+        to = owner(t * rounds)
         return (
-            pltpu.make_async_remote_copy(stage.at[step], recv.at[r, t], osend.at[step], orecv.at[r, t], device_id={"sp": to}, device_id_type=MESH),
-            pltpu.make_async_remote_copy(stage_ml.at[step], recv_ml.at[r, t], msend.at[step], mrecv.at[r, t], device_id={"sp": to}, device_id_type=MESH),
+            pltpu.make_async_remote_copy(stage.at[t], recv.at[t], osend.at[t], orecv.at[t], device_id={"sp": to}, device_id_type=MESH),
+            pltpu.make_async_remote_copy(stage_ml.at[t], recv_ml.at[t], msend.at[t], mrecv.at[t], device_id={"sp": to}, device_id_type=MESH),
         )
 
     def result_copy(r, u):
@@ -140,18 +136,17 @@
         total = jnp.sum(jnp.where(own8, total, 0.0), axis=0, keepdims=True)
         total = total + pltpu.roll(total, side, 1)
         seen = seen[0:heads, 0:head] + seen[side : side + heads, head : 2 * head]
-        stage[step] = seen.astype(BF16)
-        own_f[step & 1] = seen
-        stage_ml[step] = jnp.concatenate([high, total], axis=0)
+        r, t = place(step)
+        stage[t, r] = seen.astype(BF16)
+        own_f[r] = seen
+        stage_ml[t, r] = jnp.concatenate([high, total], axis=0)
 
     first = jnp.full((8, LANES), -jnp.inf, F32)
     zeros = (jnp.zeros((8, LANES), F32), jnp.zeros((2 * side, 2 * head), F32))
 
-    def send(step):
-        @pl.when(step < rounds * (n - 1))
-        def _():
-            for copy in part_copies(step):
-                copy.start()
+    def send(t):
+        for copy in part_copies(t):
+            copy.start()
 
     def both(step, high, qb, s, s_before):
         scores_start(step, qb)
@@ -172,27 +167,24 @@
             def _():
                 vcopy(at - 1).start()
 
-    def combine(r):
-        step = rounds * (n - 1) + r
-        for t in range(n - 2):
-            for copy in part_copies(r * (n - 1) + t):
-                copy.wait_recv()
-        high = recv_ml[r, 0 : n - 2, 0, :]
-        others = jnp.max(high, axis=0, keepdims=True)
-        share = jnp.exp2(high * scale - others * scale)
-        total = jnp.sum(share * recv_ml[r, 0 : n - 2, 1, :], axis=0, keepdims=True)
+    def far_parts(r):
+        high = recv_ml[0 : n - 2, r, 0, :]
+        highest = jnp.max(high, axis=0, keepdims=True)
+        share = jnp.exp2(high * scale - highest * scale)
+        total = jnp.sum(share * recv_ml[0 : n - 2, r, 1, :], axis=0, keepdims=True)
         share = jnp.concatenate([share, jnp.zeros((LANES - (n - 2), LANES), F32)], axis=0).T
-        seen = share[0:heads, 0:1] * recv[r, 0].astype(F32)
+        seen = share[0:heads, 0:1] * recv[0, r].astype(F32)
         for t in range(1, n - 2):
-            seen = seen + share[0:heads, t : t + 1] * recv[r, t].astype(F32)
-        for copy in part_copies(r * (n - 1) + n - 2):
-            copy.wait_recv()
-        high = jnp.concatenate([others, recv_ml[r, n - 2, 0:1, :], stage_ml[step, 0:1, :]], axis=0)
-        total = jnp.concatenate([total, recv_ml[r, n - 2, 1:2, :], stage_ml[step, 1:2, :]], axis=0)
+            seen = seen + share[0:heads, t : t + 1] * recv[t, r].astype(F32)
+        return highest, total, seen
+
+    def finish(r, high, total, seen):
+        high = jnp.concatenate([high, recv_ml[n - 2, r, 0:1, :], stage_ml[n - 1, r, 0:1, :]], axis=0)
+        total = jnp.concatenate([total, recv_ml[n - 2, r, 1:2, :], stage_ml[n - 1, r, 1:2, :]], axis=0)
         share = jnp.exp2(high * scale - jnp.max(high, axis=0, keepdims=True) * scale)
         share = share / jnp.sum(share * total, axis=0, keepdims=True)
         share = jnp.concatenate([share, jnp.zeros((LANES - 3, LANES), F32)], axis=0).T
-        seen = share[0:heads, 0:1] * seen + share[0:heads, 1:2] * recv[r, n - 2].astype(F32) + share[0:heads, 2:3] * own_f[r]
+        seen = share[0:heads, 0:1] * seen + share[0:heads, 1:2] * recv[n - 2, r].astype(F32) + share[0:heads, 2:3] * own_f[r]
         o_ref[r * n + me] = seen.astype(BF16)
         for u in range(chips):
             result_copy(r, u).start()
@@ -207,47 +199,53 @@
     for piece in range(pieces):
         high = scores_piece(0, piece, qb0, s0, high)
     high = scores_end(high)
-    pl.semaphore_wait(barrier, n - 1)
-
-    def body(trip, high):
+
+    def body(trip, high, sending):
         step = 2 * trip + 1
         kcopy(step).wait()
         vcopy(step - 1).wait()
         kcopy(step + 1).wait()
         vcopy(step).wait()
         refill(step + 5)
+
+        if sending:
+            send(trip - 1)
+
         high = both(step, high, qb1, s1, s0)
         high = both(step + 1, high, qb0, s0, s1)
 
-        @pl.when(trip >= 1)
-        def _():
-            send(step - 2)
-
-        send(step - 1)
         return high
 
-    high = lax.fori_loop(0, (seqs - 2) // 2, body, high)
-    send(seqs - 3)
+    high = lax.fori_loop(0, QUIET, functools.partial(body, sending=False), high)
+    pl.semaphore_wait(barrier, n - 1)
+    for t in range(QUIET - 1):
+        send(t)
+    high = lax.fori_loop(QUIET, (seqs - 2) // 2, functools.partial(body, sending=True), high)
+    send(n - 2)
     kcopy(seqs - 1).wait()
     vcopy(seqs - 2).wait()
     high = both(seqs - 1, high, qb1, s1, s0)
-    combine(0)
+    for t in range(n - 2):
+        for copy in part_copies(t):
+            copy.wait_recv()
+    parts = [far_parts(r) for r in range(rounds)]
+    for copy in part_copies(n - 2):
+        copy.wait_recv()
+    for r in range(rounds - 1):
+        finish(r, *parts[r])
     vcopy(seqs - 1).wait()
     total, seen = zeros
     for piece in range(pieces):
         total, seen = values_piece(seqs - 1, piece, s1, high, total, seen)
     values_end(seqs - 1, high, total, seen)
-    combine(rounds - 1)
-
-    def drain(step, _):
-        @pl.when(step < rounds * (n - 1))
-        def _():
-            for copy in part_copies(step):
-                copy.wait_send()
-
+    finish(rounds - 1, *parts[-1])
+
+    def drain(t, _):
+        for copy in part_copies(t):
+            copy.wait_send()
         return 0
 
-    lax.fori_loop(0, seqs, drain, 0)
+    lax.fori_loop(0, n - 1, drain, 0)
     for r in range(rounds):
         for u in reversed(range(chips - 1)):
             result_arrival(r, u).wait_recv()
@@ -284,18 +282,18 @@
                 pltpu.VMEM((rows // 2, LANES), F32),
                 pltpu.VMEM((LANES, 2 * head), BF16),
                 pltpu.VMEM((LANES, 2 * head), BF16),
-                pltpu.VMEM((seqs, heads, head), BF16),
-                pltpu.VMEM((seqs, 2, LANES), F32),
+                pltpu.VMEM((n, rounds, heads, head), BF16),
+                pltpu.VMEM((n, rounds, 2, LANES), F32),
                 pltpu.VMEM((rounds, heads, head), F32),
-                pltpu.VMEM((rounds, n, heads, head), BF16),
-                pltpu.VMEM((rounds, n, 2, LANES), F32),
+                pltpu.VMEM((n, rounds, heads, head), BF16),
+                pltpu.VMEM((n, rounds, 2, LANES), F32),
                 dma,
                 dma((SLOTS,)),
                 dma((SLOTS,)),
-                dma((seqs,)),
-                dma((rounds, n)),
-                dma((seqs,)),
-                dma((rounds, n)),
+                dma((n,)),
+                dma((n,)),
+                dma((n,)),
+                dma((n,)),
                 dma((rounds, n // 2)),
                 dma((rounds, n // 2)),
                 dma((rounds, n // 2)),

time: 40.6 us -> 40.1 us (0.988)
  Pallas kernels: 39.7 us -> 39.2 us
    pallas_call x1, Pallas kernels: 39.7 us -> 39.2 us  [step(): pl.pallas_call(functools.partial(kernel, n, key_heads), out_shape=jax.Sha...]
where the time goes in v5:
time: 40.1 us; the launch traced here: 40 us
  Pallas kernels  39.2 us (98%)
  local copies, waits for them, and re-layouts  0.77 us (2%)
    pallas_call x1, Pallas kernels, step(): pl.pallas_call(functools.partial(kernel, n, key_heads), out_shape=jax.Sha...  39.2 us

profile of v5, /device:TPU:21, one launch (start us, length us, event | category | flops | bytes accessed | tf_op | source)
XLA Modules:
  0.0 40.0 jit_solution(203680663172818993)
XLA Ops:
  0.0 39.2 %shard_map.37 = bf16[32,56,128]{2,1,0:T(8,128)(2,1)S(1)} custom-call(bf16[32,56,128]{2,1,0:T(8,128)(2,1)} %q_hbm.1, bf16[32,4096,128]{2,1,0:T(8,128)(2,1)} %bitcast.2, bf16[32,4096,128]{2,1,0:T(8,128)(2,1)} %bitcast.3), custom_call_target="tpu_custom_call" | custom-call | tf_op jit(solution)/shard_map/pallas_call | solution.py:272
  39.2 0.8 %copy.5 = bf16[32,56,128]{2,1,0:T(8,128)(2,1)} copy(bf16[32,56,128]{2,1,0:T(8,128)(2,1)S(1)} %shard_map.37) | data formatting | bytes 917504

commit v6 on v5

--- a/solution.py
+++ b/solution.py
@@ -40,7 +40,7 @@
 
     def ahead(u):
         near, odd = (u // 2, u % 2) if isinstance(u, int) else (whole(u, 2), rest(u, 2))
-        return chips // 2 + near - (2 * near + 1) * odd
+        return chips // 2 - near + (2 * near + 1) * odd
 
     def device(dz, other):
         return 2 * rest(whole(me, 2) + dz, chips) + rest(rest(me, 2) + other, 2)

time: 40.1 us -> 39.9 us (level)
  no operation moved by 1% of the time
where the time goes in v6:
time: 39.9 us
  Pallas kernels  39.1 us (98%)
  local copies, waits for them, and re-layouts  0.77 us (2%)
    pallas_call x1, Pallas kernels, step(): pl.pallas_call(functools.partial(kernel, n, key_heads), out_shape=jax.Sha...  39.1 us

profile of v6, /device:TPU:21, one launch (start us, length us, event | category | flops | bytes accessed | tf_op | source)
XLA Modules:
  0.0 39.9 jit_solution(5928820430218262875)
XLA Ops:
  0.0 39.1 %shard_map.37 = bf16[32,56,128]{2,1,0:T(8,128)(2,1)S(1)} custom-call(bf16[32,56,128]{2,1,0:T(8,128)(2,1)} %q_hbm.1, bf16[32,4096,128]{2,1,0:T(8,128)(2,1)} %bitcast.2, bf16[32,4096,128]{2,1,0:T(8,128)(2,1)} %bitcast.3), custom_call_target="tpu_custom_call" | custom-call | tf_op jit(solution)/shard_map/pallas_call | solution.py:272
  39.1 0.8 %copy.5 = bf16[32,56,128]{2,1,0:T(8,128)(2,1)} copy(bf16[32,56,128]{2,1,0:T(8,128)(2,1)S(1)} %shard_map.37) | data formatting | bytes 917504
